TPU v7x, 256 devices: a whole 4x4x8 slice. The times are simulated.
256 devices in a mesh: dp: 16 (over y, x), expert: 8 (over z), tensor: 2 (over core).
Axes of the slice: x: 4, y: 4, z: 8, core: 2. Of those that a mesh axis runs over, the one named last changes fastest.
Arguments:
- tokens: bfloat16 [2048, 4096], P(('dp', 'expert'), 'tensor'), may hold values from -6 to 6
- target: bfloat16 [2048, 4096], P(('dp', 'expert'), 'tensor'), may hold values from -4 to 4
- router: bfloat16 [4096, 8], P('tensor'), may hold values from -1 to 1
- w_gate: bfloat16 [8, 4096, 14336], P('expert', None, ('dp', 'tensor')), may hold values from -1 to 1
- w_up: bfloat16 [8, 4096, 14336], P('expert', None, ('dp', 'tensor')), may hold values from -1 to 1
- w_down: bfloat16 [8, 14336, 4096], P('expert', ('dp', 'tensor')), may hold values from -1 to 1
- expert_ids: int32 [2048, 2], P(('dp', 'expert')), may hold values from 0 to 7, as said below
- lengths: int32 [64], replicated, may hold values from 1 to 128, 2048 in all
- bench_ids: int32 [64], replicated, may hold values from 0 to 15
Outputs:
- mixed: bfloat16 [2048, 4096], P(('dp', 'expert'), 'tensor')
- bench_loss: float32 [16], replicated
- counts: int32 [16], replicated
Inputs may be any that keep to these rules, and one draw needn't show every extreme that they name: `expert_ids`: each row names two different experts; among the 16 rows of one device no expert is named by more than 8 rows; for each index of dp, one expert is named by exactly 8 rows of every device of that index. The lengths sum to 2048.
All inputs are finite; a program needn't handle non-finite values.
Results may differ from a plain program's by a relative error of at most 0.0085.
Values may be sent and summed in bfloat16 or wider, within the bound.
A program may use at most 128 MiB of HBM per device.

v0:
```python
import jax
import jax.numpy as jnp
from jax import lax
from jax.sharding import Mesh
from jax.sharding import PartitionSpec as P

D = 4096
NB = 16
CAP = 8
DP = ("dp_0", "dp_1")
DP_EXPERT = ("dp_0", "dp_1", "expert")
DP_EXPERT_TENSOR = ("dp_0", "dp_1", "expert", "tensor")
DP_TENSOR = ("dp_0", "dp_1", "tensor")


def cut_along(shard, dim, size):
    before, after = (shard.shape[:dim], shard.shape[dim + 1 :])
    return jnp.moveaxis(shard.reshape(*before, size, -1, *after), dim, 0)


def sent_and_summed(shard, axis, dim):
    pieces = cut_along(shard, dim, lax.axis_size(axis))
    arrived = lax.all_to_all(pieces, axis, split_axis=0, concat_axis=0, tiled=True)
    return arrived.sum(axis=0)


def one_axis_at_a_time(shard, axes):
    for axis in axes:
        shard = lax.psum(shard, axis)
    return shard


def per_device(tokens, target, router, w_gate, w_up, w_down, expert_ids, lengths, bench_ids):
    tensor_count = lax.axis_size("tensor")
    local_tokens = tokens.shape[0]
    experts = router.shape[1]
    half_cap = CAP // tensor_count
    slot_rows = tensor_count * experts * half_cap
    partial_value = jnp.dot(tokens, router, preferred_element_type=jnp.float32)
    logits = lax.psum(partial_value, "tensor")
    chosen = expert_ids[:, :, None] == jnp.arange(experts, dtype=jnp.int32)[None, None, :]
    picked = jnp.sum(jnp.where(chosen, logits[:, None, :], jnp.float32(0.0)), axis=2)
    gates = jnp.stack(
        [jax.nn.sigmoid(picked[:, 0] - picked[:, 1]), jax.nn.sigmoid(picked[:, 1] - picked[:, 0])],
        axis=1,
    )
    marks = chosen.reshape(local_tokens * 2, experts).astype(jnp.int32)
    before = jnp.cumsum(marks, axis=0) - marks
    slot = jnp.sum(before * marks, axis=1)
    flat_ids = expert_ids.reshape(local_tokens * 2)
    target_row = slot // half_cap * (experts * half_cap) + flat_ids * half_cap + slot % half_cap
    placing = (target_row[None, :] == jnp.arange(slot_rows, dtype=jnp.int32)[:, None]).reshape(
        slot_rows, local_tokens, 2
    )
    dispatch_map = jnp.any(placing, axis=2).astype(jnp.bfloat16)
    outgoing = jnp.dot(dispatch_map, tokens, preferred_element_type=jnp.float32).astype(
        jnp.bfloat16
    )
    outgoing = outgoing.reshape(tensor_count, experts, half_cap, tokens.shape[1])
    arrived = lax.all_to_all(outgoing, "expert", split_axis=1, concat_axis=1, tiled=True)
    whole = lax.all_gather(arrived, "tensor", axis=3, tiled=True)
    whole = whole.reshape(1, slot_rows, D)
    every_row = lax.all_gather(whole, DP, axis=0, tiled=True).reshape(-1, D)
    gate_w = w_gate[0]
    up_w = w_up[0]
    down_w = w_down[0]
    gate = jnp.dot(every_row, gate_w, preferred_element_type=jnp.float32)
    up = jnp.dot(every_row, up_w, preferred_element_type=jnp.float32)
    hidden = (jax.nn.silu(gate) * up).astype(jnp.bfloat16)
    summed = lax.psum_scatter(
        jnp.dot(hidden, down_w, preferred_element_type=jnp.float32),
        DP,
        scatter_dimension=0,
        tiled=True,
    )
    summed = sent_and_summed(summed, "tensor", 1)
    results = summed.astype(jnp.bfloat16).reshape(
        tensor_count, experts, half_cap, D // tensor_count
    )
    returned = lax.all_to_all(results, "expert", split_axis=1, concat_axis=1, tiled=True)
    weights = jnp.einsum("rtk,tk->tr", placing.astype(jnp.float32), gates)
    flat_back = returned.reshape(slot_rows, -1).astype(jnp.float32)
    mixed = jnp.dot(weights, flat_back, precision=lax.Precision.HIGHEST).astype(jnp.bfloat16)
    first_index = lax.axis_index(DP_EXPERT) * local_tokens
    position = first_index + jnp.arange(local_tokens, dtype=jnp.int32)
    ends = jnp.cumsum(lengths)
    starts = ends - lengths
    inside = ((position[:, None] >= starts[None, :]) & (position[:, None] < ends[None, :])).astype(
        jnp.float32
    )
    closing = jnp.any((position + 1)[:, None] == ends[None, :], axis=1)
    scored = jnp.where(closing, jnp.float32(0.0), jnp.float32(1.0))
    bench_table = bench_ids[:, None] == jnp.arange(NB, dtype=jnp.int32)[None, :]
    bench_of = jnp.dot(inside, bench_table.astype(jnp.float32), precision=lax.Precision.HIGHEST)
    diff = mixed.astype(jnp.float32) - target.astype(jnp.float32)
    token_part = jnp.sum(diff * diff, axis=1) / D
    local_sums = jnp.dot(scored * token_part, bench_of, precision=lax.Precision.HIGHEST)
    loss_sum = one_axis_at_a_time(local_sums, DP_EXPERT_TENSOR)
    counts = jnp.sum(jnp.where(bench_table, (lengths - 1)[:, None], 0), axis=0)
    bench_loss = loss_sum / jnp.maximum(counts, 1).astype(jnp.float32)
    return (mixed, bench_loss, counts)


def solution(mesh):
    split = Mesh(
        mesh.devices.reshape(4, 4, mesh.shape["expert"], mesh.shape["tensor"]),
        ("dp_0", "dp_1", "expert", "tensor"),
    )
    in_specs = (
        P(DP_EXPERT, "tensor"),
        P(DP_EXPERT, "tensor"),
        P("tensor", None),
        P("expert", None, DP_TENSOR),
        P("expert", None, DP_TENSOR),
        P("expert", DP_TENSOR, None),
        P(DP_EXPERT, None),
        P(),
        P(),
    )
    out_specs = (P(DP_EXPERT, "tensor"), P(), P())
    return jax.shard_map(
        per_device, mesh=split, in_specs=in_specs, out_specs=out_specs, check_vma=False
    )
```

profile of v0, /device:TPU:1, one launch (start us, length us, event | category | flops | bytes accessed | tf_op | source)
XLA Modules:
  0.0 317.1 jit_solution(9953797493856227956)
XLA Ops:
  7.2 0.8 copy.53
  8.0 0.1 eq.64
  8.1 0.1 fusion.13
  8.1 0.1 reduce_window_sum.18
  8.2 0.2 select_reduce_fusion
  8.4 0.1 reduce_sum.48
  8.5 0.1 copy.54
  8.6 0.7 fusion.22
  9.3 0.1 fusion.34
  9.4 0.3 convolution_convert_fusion
  9.6 0.1 reshape.108
  9.7 0.1 copy.58
  9.8 19.3 %all_to_all.15 = bf16[2,8,4,2048]{3,2,0,1:T(4,128)(2,1)S(1)} all-to-all(bf16[2,8,4,2048]{3,2,0,1:T(4,128)(2,1)S(1)} %copy.58), channel_id=1, replica_groups=mesh['dp_0'=4,'dp_1'=4,'expert'=8,'tensor'=2] {'expert'}, dimensions={1} | all-to-all | bytes 524288 | tf_op jit(solution)/shard_map/all_to_all | solution.py:60
  29.2 4.1 %all_gather.6 = bf16[2,8,4,4096]{3,2,0,1:T(4,128)(2,1)S(1)} all-gather(bf16[2,8,4,2048]{3,2,0,1:T(4,128)(2,1)S(1)} %all_to_all.15), channel_id=1, replica_groups=mesh['dp_0'=4,'dp_1'=4,'expert'=8,'tensor'=2] {'tensor'}, dimensions={3}, use_global_device_ids=true | all-gather | bytes 786432 | tf_op jit(solution)/shard_map/all_gather | solution.py:61
  33.3 0.2 copy.59
  33.5 0.9 reshape.109
  34.4 0.0 reduce-scatter.2.cloned.1.call-start
  34.5 71.8 %all-gather.2.cloned.1.call-done = bf16[16,64,4096]{2,1,0:T(8,128)(2,1)} async-done(((bf16[1,64,4096]{2,1,0:T(8,128)(2,1)}), bf16[16,64,4096]{2,1,0:T(8,128)(2,1)}) %all-gather.2.cloned.1.call-update) | async-done | bytes 8388624 | tf_op jit(solution)/shard_map/all_gather | solution.py:63
  106.3 7.5 %fusion.4 = f32[1024,448]{0,1:T(8,128)S(1)} fusion(bf16[1024,4096]{1,0:T(8,128)(2,1)} %bitcast.45, bf16[1,4096,448]{1,2,0:T(8,128)(2,1)} %param.12), kind=kOutput, calls=%fused_computation.4 | convolution fusion | flops 3758096384 | bytes 13893632 | tf_op jit(solution)/shard_map/dot_general | solution.py:67
  113.8 16.5 %fusion = f32[1024,4096]{1,0:T(8,128)} fusion(bf16[1,448,4096]{2,1,0:T(8,128)(2,1)} %param.14, f32[1024,448]{0,1:T(8,128)S(1)} %fusion.4, bf16[1024,4096]{1,0:T(8,128)(2,1)} %bitcast.46, bf16[1,4096,448]{1,2,0:T(8,128)(2,1)} %param.13), kind=kOutput, calls=%fused_computation | convolution fusion | flops 7518945280 | bytes 34340864 | tf_op jit(solution)/shard_map/dot_general | solution.py:71
  130.4 0.6 copy-done.4
  131.0 0.1 copy.63
  131.1 0.1 reduce-window.8
  131.2 0.1 reduce
  131.3 0.1 fusion.35
  131.4 3.0 psum.35
  134.4 0.1 select_reduce_fusion.1
  134.5 0.2 compare_reduce_fusion
  134.7 111.3 %reduce-scatter.2.cloned.1.call-done = f32[64,4096]{1,0:T(8,128)} async-done(((f32[1024,4096]{1,0:T(8,128)}), f32[64,4096]{1,0:T(8,128)}) %reduce-scatter.2.cloned.1.call-update) | async-done | bytes 1048592 | tf_op jit(solution)/shard_map/reduce_scatter | solution.py:70
  246.0 1.3 copy.71
  247.3 5.1 %all_to_all.16 = f32[2,64,2048]{2,1,0:T(8,128)S(1)} all-to-all(f32[2,64,2048]{2,1,0:T(8,128)S(1)} %bitcast.41), channel_id=1, replica_groups=mesh['dp_0'=4,'dp_1'=4,'expert'=8,'tensor'=2] {'tensor'}, dimensions={0} | all-to-all | bytes 2097152 | tf_op jit(solution)/shard_map/all_to_all | solution.py:23
  252.4 0.1 reduce_sum.50
  252.5 0.1 convert_element_type.37
  252.6 0.8 copy.61
  253.4 6.8 %all-to-all-start.2 = ((bf16[2,8,4,2048]{3,2,0,1:T(4,128)(2,1)}), bf16[2,8,4,2048]{3,2,0,1:T(4,128)(2,1)S(1)}, u32[]{:S(2)}, u32[]{:S(2)}) async-start(bf16[2,8,4,2048]{3,2,0,1:T(4,128)(2,1)} %copy.61), calls=%async_computation.3 | async-start | bytes 524288 | tf_op jit(solution)/shard_map/all_to_all | solution.py:80
  260.2 0.1 copy.65
  260.3 0.2 fusion.14
  260.5 0.1 fusion.11
  260.6 10.7 %all-to-all-done.2 = bf16[2,8,4,2048]{3,2,0,1:T(4,128)(2,1)S(1)} async-done(((bf16[2,8,4,2048]{3,2,0,1:T(4,128)(2,1)}), bf16[2,8,4,2048]{3,2,0,1:T(4,128)(2,1)S(1)}, u32[]{:S(2)}, u32[]{:S(2)}) %all-to-all-start.2) | async-done | bytes 262176 | tf_op jit(solution)/shard_map/all_to_all | solution.py:80
  271.3 0.1 copy.62
  271.4 0.1 reshape.112
  271.5 1.0 multiply_reduce_fusion
  272.4 0.1 convolution_bitcast_fusion
  272.6 8.0 %psum.36 = f32[16]{0:T(128)S(1)} all-reduce(f32[16]{0:T(128)S(1)} %convolution_bitcast_fusion), channel_id=1, replica_groups=mesh['dp_0'=4,'dp_1'=4,'expert'=8,'tensor'=2] {'dp_0'}, use_global_device_ids=true, to_apply=%region_10.11 | all-reduce | flops 16 | bytes 128 | tf_op jit(solution)/shard_map/psum | solution.py:29
  280.5 6.7 %psum.37 = f32[16]{0:T(128)S(1)} all-reduce(f32[16]{0:T(128)S(1)} %psum.36), channel_id=1, replica_groups=mesh['dp_0'=4,'dp_1'=4,'expert'=8,'tensor'=2] {'dp_1'}, use_global_device_ids=true, to_apply=%region_11.12 | all-reduce | flops 16 | bytes 128 | tf_op jit(solution)/shard_map/psum | solution.py:29
  287.2 10.7 %psum.38 = f32[16]{0:T(128)S(1)} all-reduce(f32[16]{0:T(128)S(1)} %psum.37), channel_id=1, replica_groups=mesh['dp_0'=4,'dp_1'=4,'expert'=8,'tensor'=2] {'expert'}, use_global_device_ids=true, to_apply=%region_12.13 | all-reduce | flops 16 | bytes 128 | tf_op jit(solution)/shard_map/psum | solution.py:29
  297.9 11.9 %psum.39 = f32[16]{0:T(128)S(1)} all-reduce(f32[16]{0:T(128)S(1)} %psum.38), channel_id=1, replica_groups=mesh['dp_0'=4,'dp_1'=4,'expert'=8,'tensor'=2] {'tensor'}, use_global_device_ids=true, to_apply=%region_13.14 | all-reduce | flops 16 | bytes 128 | tf_op jit(solution)/shard_map/psum | solution.py:29
  309.8 0.5 convert_divide_fusion
  (21 shorter events, 0.2 us)
Async XLA Ops:
  7.2 2.2 copy-start
  7.2 99.1 %all-gather.2.cloned.1.call-start = ((), (), s32[]{:S(2)}) async-start(), calls=%async_computation.4 | async-start | bytes 8912896 | tf_op jit(solution)/shard_map/all_gather | solution.py:63
  34.4 211.6 %reduce-scatter.2.cloned.1.call-start = ((), (), s32[]{:S(2)}) async-start(), calls=%async_computation.5 | async-start | bytes 17825792 | tf_op jit(solution)/shard_map/reduce_scatter | solution.py:70
  130.3 0.7 copy-start.4
  130.3 1.0 copy-start.2
  130.3 4.1 %copy-start.5 = (s32[64]{0:T(128)S(1)}, s32[64]{0:T(128)}, u32[]{:S(2)}) copy-start(s32[64]{0:T(128)} %param.17) | copy-start | bytes 772
  130.3 4.2 %copy-start.3 = (s32[16,2]{0,1:T(2,128)S(1)}, s32[16,2]{0,1:T(2,128)}, u32[]{:S(2)}) copy-start(s32[16,2]{0,1:T(2,128)} %param.15) | copy-start | bytes 388
  134.5 175.3 %copy-start.6 = (s32[16]{0:T(128)}, s32[16]{0:T(128)S(1)}, u32[]{:S(2)}) copy-start(s32[16]{0:T(128)S(1)} %select_reduce_fusion.1) | copy-start | bytes 196
  246.0 25.5 %copy-start.1 = (bf16[16,2048]{1,0:T(8,128)(2,1)S(1)}, bf16[16,2048]{1,0:T(8,128)(2,1)}, u32[]{:S(2)}) copy-start(bf16[16,2048]{1,0:T(8,128)(2,1)} %param.10) | copy-start | bytes 196612
  253.4 17.9 %all-to-all-start.2 = ((bf16[2,8,4,2048]{3,2,0,1:T(4,128)(2,1)}), bf16[2,8,4,2048]{3,2,0,1:T(4,128)(2,1)S(1)}, u32[]{:S(2)}, u32[]{:S(2)}) async-start(bf16[2,8,4,2048]{3,2,0,1:T(4,128)(2,1)} %copy.61), calls=%async_computation.3 | async-start | bytes 524288 | tf_op jit(solution)/shard_map/all_to_all | solution.py:80
Sparse Core Ops, SparseCore 0:
  34.5 71.6 all-gather.1
  130.5 115.4 reduce-scatter.1
where the time goes:
time: 318 us; the launch traced here: 317 us
  waiting for transfers between devices  194 us (61%)
  blocking collectives  68.7 us (22%)
  matrix products  25.9 us (8%)
  between operations  14.2 us (4%)
  starting transfers between devices  6.86 us (2%)
  local copies, waits for them, and re-layouts  5.59 us (2%)
    reduce_scatter x1, waiting for transfers between devices, per_device(): lax.psum_scatter(jnp.dot(hidden, down_w, preferred_element_type=jnp.float...  111 us
    all_gather x1, waiting for transfers between devices, per_device(): every_row = lax.all_gather(whole, DP, axis=0, tiled=True).reshape(-1, D)  71.8 us
    psum x4, blocking collectives, one_axis_at_a_time(): shard = lax.psum(shard, axis)  37.2 us
    all_to_all x1, blocking collectives, per_device(): lax.all_to_all(outgoing, 'expert', split_axis=1, concat_axis=1, tiled=True)  19.3 us
    dot_general x1, matrix products, per_device(): jnp.dot(hidden, down_w, preferred_element_type=jnp.float32)  16.5 us
    all_to_all x1, waiting for transfers between devices, per_device(): lax.all_to_all(results, 'expert', split_axis=1, concat_axis=1, tiled=True)  10.7 us
    dot_general x1, matrix products, per_device(): gate = jnp.dot(every_row, gate_w, preferred_element_type=jnp.float32)  7.52 us
    all_to_all x1, starting transfers between devices, per_device(): lax.all_to_all(results, 'expert', split_axis=1, concat_axis=1, tiled=True)  6.78 us
  transfers between devices with their start and end apart: 3, of which 3 were waited for; matrix products, arithmetic and copies ran while one was open for 0% of the time, Pallas kernels for 0%

commit v1 on v0

--- a/solution.py
+++ b/solution.py
@@ -77,7 +77,12 @@
     results = summed.astype(jnp.bfloat16).reshape(
         tensor_count, experts, half_cap, D // tensor_count
     )
-    returned = lax.all_to_all(results, "expert", split_axis=1, concat_axis=1, tiled=True)
+    returned = jnp.concatenate(
+        lax.all_to_all(
+            jnp.stack(jnp.split(results, lax.axis_size("expert"), axis=1)), "expert", 0, 0
+        ),
+        axis=1,
+    )
     weights = jnp.einsum("rtk,tk->tr", placing.astype(jnp.float32), gates)
     flat_back = returned.reshape(slot_rows, -1).astype(jnp.float32)
     mixed = jnp.dot(weights, flat_back, precision=lax.Precision.HIGHEST).astype(jnp.bfloat16)

time: 318 us -> 322 us (1.013)
  local copies, waits for them, and re-layouts: 5.59 us -> 9.71 us
    unnamed x15 -> x22, local copies, waits for them, and re-layouts: 1.4 us -> 5.7 us
where the time goes in v1:
time: 322 us; the launch traced here: 321 us
  waiting for transfers between devices  194 us (60%)
  blocking collectives  68.7 us (21%)
  matrix products  25.9 us (8%)
  between operations  14.2 us (4%)
  local copies, waits for them, and re-layouts  9.71 us (3%)
  starting transfers between devices  6.86 us (2%)
    reduce_scatter x1, waiting for transfers between devices, per_device(): lax.psum_scatter(jnp.dot(hidden, down_w, preferred_element_type=jnp.float...  111 us
    all_gather x1, waiting for transfers between devices, per_device(): every_row = lax.all_gather(whole, DP, axis=0, tiled=True).reshape(-1, D)  71.8 us
    psum x4, blocking collectives, one_axis_at_a_time(): shard = lax.psum(shard, axis)  37.2 us
    all_to_all x1, blocking collectives, per_device(): lax.all_to_all(outgoing, 'expert', split_axis=1, concat_axis=1, tiled=True)  19.3 us
    dot_general x1, matrix products, per_device(): jnp.dot(hidden, down_w, preferred_element_type=jnp.float32)  16.5 us
    all_to_all x1, waiting for transfers between devices, per_device(): lax.all_to_all(jnp.stack(jnp.split(results, lax.axis_size('expert'), axis...  10.7 us
    dot_general x1, matrix products, per_device(): gate = jnp.dot(every_row, gate_w, preferred_element_type=jnp.float32)  7.52 us
    all_to_all x1, starting transfers between devices, per_device(): lax.all_to_all(jnp.stack(jnp.split(results, lax.axis_size('expert'), axis...  6.78 us
  transfers between devices with their start and end apart: 3, of which 3 were waited for; matrix products, arithmetic and copies ran while one was open for 0% of the time, Pallas kernels for 0%

profile of v1, /device:TPU:1, one launch (start us, length us, event | category | flops | bytes accessed | tf_op | source)
XLA Modules:
  0.0 321.2 jit_solution(4121336262141172511)
XLA Ops:
  7.2 0.8 copy.101
  8.0 0.1 eq.64
  8.2 0.2 select_reduce_fusion
  8.5 0.1 copy.102
  8.6 0.7 fusion.30
  9.4 0.3 convolution_convert_fusion
  9.6 0.1 reshape.108
  9.7 0.1 copy.106
  9.8 19.3 %all_to_all.15 = bf16[2,8,4,2048]{3,2,0,1:T(4,128)(2,1)S(1)} all-to-all(bf16[2,8,4,2048]{3,2,0,1:T(4,128)(2,1)S(1)} %copy.106), channel_id=1, replica_groups=mesh['dp_0'=4,'dp_1'=4,'expert'=8,'tensor'=2] {'expert'}, dimensions={1} | all-to-all | bytes 524288 | tf_op jit(solution)/shard_map/all_to_all | solution.py:60
  29.2 4.1 %all_gather.6 = bf16[2,8,4,4096]{3,2,0,1:T(4,128)(2,1)S(1)} all-gather(bf16[2,8,4,2048]{3,2,0,1:T(4,128)(2,1)S(1)} %all_to_all.15), channel_id=1, replica_groups=mesh['dp_0'=4,'dp_1'=4,'expert'=8,'tensor'=2] {'tensor'}, dimensions={3}, use_global_device_ids=true | all-gather | bytes 786432 | tf_op jit(solution)/shard_map/all_gather | solution.py:61
  33.3 0.2 copy.107
  33.5 0.9 reshape.109
  34.5 71.8 %all-gather.2.cloned.1.call-done = bf16[16,64,4096]{2,1,0:T(8,128)(2,1)} async-done(((bf16[1,64,4096]{2,1,0:T(8,128)(2,1)}), bf16[16,64,4096]{2,1,0:T(8,128)(2,1)}) %all-gather.2.cloned.1.call-update) | async-done | bytes 8388624 | tf_op jit(solution)/shard_map/all_gather | solution.py:63
  106.3 7.5 %fusion.4 = f32[1024,448]{0,1:T(8,128)S(1)} fusion(bf16[1024,4096]{1,0:T(8,128)(2,1)} %bitcast.95, bf16[1,4096,448]{1,2,0:T(8,128)(2,1)} %param.12), kind=kOutput, calls=%fused_computation.4 | convolution fusion | flops 3758096384 | bytes 13893632 | tf_op jit(solution)/shard_map/dot_general | solution.py:67
  113.8 16.5 %fusion = f32[1024,4096]{1,0:T(8,128)} fusion(bf16[1,448,4096]{2,1,0:T(8,128)(2,1)} %param.14, f32[1024,448]{0,1:T(8,128)S(1)} %fusion.4, bf16[1024,4096]{1,0:T(8,128)(2,1)} %bitcast.96, bf16[1,4096,448]{1,2,0:T(8,128)(2,1)} %param.13), kind=kOutput, calls=%fused_computation | convolution fusion | flops 7518945280 | bytes 34340864 | tf_op jit(solution)/shard_map/dot_general | solution.py:71
  130.4 0.6 copy-done.4
  131.0 0.1 copy.117
  131.1 0.1 reduce-window.8
  131.2 0.1 reduce
  131.3 0.1 fusion.43
  131.4 3.0 psum.35
  134.4 0.1 select_reduce_fusion.1
  134.5 0.2 compare_reduce_fusion
  134.7 111.2 %reduce-scatter.2.cloned.1.call-done = f32[64,4096]{1,0:T(8,128)} async-done(((f32[1024,4096]{1,0:T(8,128)}), f32[64,4096]{1,0:T(8,128)}) %reduce-scatter.2.cloned.1.call-update) | async-done | bytes 1048592 | tf_op jit(solution)/shard_map/reduce_scatter | solution.py:70
  246.0 1.3 copy.132
  247.3 5.1 %all_to_all.16 = f32[2,64,2048]{2,1,0:T(8,128)S(1)} all-to-all(f32[2,64,2048]{2,1,0:T(8,128)S(1)} %bitcast.90), channel_id=1, replica_groups=mesh['dp_0'=4,'dp_1'=4,'expert'=8,'tensor'=2] {'tensor'}, dimensions={0} | all-to-all | bytes 2097152 | tf_op jit(solution)/shard_map/all_to_all | solution.py:23
  252.5 0.1 convert_element_type.37
  252.6 0.6 fusion.18
  253.2 0.6 fusion.17
  253.8 0.6 fusion.16
  254.4 0.6 fusion.15
  255.0 0.6 fusion.14
  255.7 0.6 fusion.13
  256.3 0.6 fusion.12
  256.9 0.6 fusion.11
  257.5 6.8 %all-to-all-start.2 = ((bf16[8,2,1,4,2048]{4,3,1,2,0:T(4,128)(2,1)}), bf16[8,2,1,4,2048]{4,3,1,2,0:T(4,128)(2,1)S(1)}, u32[]{:S(2)}, u32[]{:S(2)}) async-start(bf16[8,2,1,4,2048]{4,3,1,2,0:T(4,128)(2,1)} %fusion.11), calls=%async_computation.3 | async-start | bytes 524288 | tf_op jit(solution)/shard_map/all_to_all | solution.py:81
  264.3 0.1 copy.119
  264.4 0.2 fusion.22
  264.6 0.1 fusion.19
  264.7 10.7 %all-to-all-done.2 = bf16[8,2,1,4,2048]{4,3,1,2,0:T(4,128)(2,1)S(1)} async-done(((bf16[8,2,1,4,2048]{4,3,1,2,0:T(4,128)(2,1)}), bf16[8,2,1,4,2048]{4,3,1,2,0:T(4,128)(2,1)S(1)}, u32[]{:S(2)}, u32[]{:S(2)}) %all-to-all-start.2) | async-done | bytes 262176 | tf_op jit(solution)/shard_map/all_to_all | solution.py:81
  275.4 0.1 copy.116
  275.6 1.0 multiply_reduce_fusion
  276.6 0.1 convolution_bitcast_fusion
  276.7 8.0 %psum.36 = f32[16]{0:T(128)S(1)} all-reduce(f32[16]{0:T(128)S(1)} %convolution_bitcast_fusion), channel_id=1, replica_groups=mesh['dp_0'=4,'dp_1'=4,'expert'=8,'tensor'=2] {'dp_0'}, use_global_device_ids=true, to_apply=%region_10.11 | all-reduce | flops 16 | bytes 128 | tf_op jit(solution)/shard_map/psum | solution.py:29
  284.6 6.7 %psum.37 = f32[16]{0:T(128)S(1)} all-reduce(f32[16]{0:T(128)S(1)} %psum.36), channel_id=1, replica_groups=mesh['dp_0'=4,'dp_1'=4,'expert'=8,'tensor'=2] {'dp_1'}, use_global_device_ids=true, to_apply=%region_11.12 | all-reduce | flops 16 | bytes 128 | tf_op jit(solution)/shard_map/psum | solution.py:29
  291.3 10.7 %psum.38 = f32[16]{0:T(128)S(1)} all-reduce(f32[16]{0:T(128)S(1)} %psum.37), channel_id=1, replica_groups=mesh['dp_0'=4,'dp_1'=4,'expert'=8,'tensor'=2] {'expert'}, use_global_device_ids=true, to_apply=%region_12.13 | all-reduce | flops 16 | bytes 128 | tf_op jit(solution)/shard_map/psum | solution.py:29
  302.0 11.9 %psum.39 = f32[16]{0:T(128)S(1)} all-reduce(f32[16]{0:T(128)S(1)} %psum.38), channel_id=1, replica_groups=mesh['dp_0'=4,'dp_1'=4,'expert'=8,'tensor'=2] {'tensor'}, use_global_device_ids=true, to_apply=%region_13.14 | all-reduce | flops 16 | bytes 128 | tf_op jit(solution)/shard_map/psum | solution.py:29
  313.9 0.5 convert_divide_fusion
  (28 shorter events, 0.6 us)
Async XLA Ops:
  7.2 2.2 copy-start
  7.2 99.1 %all-gather.2.cloned.1.call-start = ((), (), s32[]{:S(2)}) async-start(), calls=%async_computation.4 | async-start | bytes 8912896 | tf_op jit(solution)/shard_map/all_gather | solution.py:63
  34.4 211.6 %reduce-scatter.2.cloned.1.call-start = ((), (), s32[]{:S(2)}) async-start(), calls=%async_computation.5 | async-start | bytes 17825792 | tf_op jit(solution)/shard_map/reduce_scatter | solution.py:70
  130.3 0.7 copy-start.4
  130.3 1.0 copy-start.2
  130.3 4.1 %copy-start.5 = (s32[64]{0:T(128)S(1)}, s32[64]{0:T(128)}, u32[]{:S(2)}) copy-start(s32[64]{0:T(128)} %param.17) | copy-start | bytes 772
  130.3 4.2 %copy-start.3 = (s32[16,2]{0,1:T(2,128)S(1)}, s32[16,2]{0,1:T(2,128)}, u32[]{:S(2)}) copy-start(s32[16,2]{0,1:T(2,128)} %param.15) | copy-start | bytes 388
  134.5 179.4 %copy-start.6 = (s32[16]{0:T(128)}, s32[16]{0:T(128)S(1)}, u32[]{:S(2)}) copy-start(s32[16]{0:T(128)S(1)} %select_reduce_fusion.1) | copy-start | bytes 196
  246.0 29.6 %copy-start.1 = (bf16[16,2048]{1,0:T(8,128)(2,1)S(1)}, bf16[16,2048]{1,0:T(8,128)(2,1)}, u32[]{:S(2)}) copy-start(bf16[16,2048]{1,0:T(8,128)(2,1)} %param.10) | copy-start | bytes 196612
  257.5 17.9 %all-to-all-start.2 = ((bf16[8,2,1,4,2048]{4,3,1,2,0:T(4,128)(2,1)}), bf16[8,2,1,4,2048]{4,3,1,2,0:T(4,128)(2,1)S(1)}, u32[]{:S(2)}, u32[]{:S(2)}) async-start(bf16[8,2,1,4,2048]{4,3,1,2,0:T(4,128)(2,1)} %fusion.11), calls=%async_computation.3 | async-start | bytes 524288 | tf_op jit(solution)/shard_map/all_to_all | solution.py:81
Sparse Core Ops, SparseCore 0:
  34.5 71.6 all-gather.1
  130.5 115.4 reduce-scatter.1
